TPU v7x, 256 devices: a whole 4x4x8 slice. The times are simulated.
256 devices in a mesh: grp: 16 (over y, z_lo, core), sp: 16 (over z_hi, x).
Axes of the slice: x: 4, y: 4, z: 8 (z_hi: 4, z_lo: 2; z = z_hi * 2 + z_lo), core: 2. Of those that a mesh axis runs over, the one named last changes fastest.
Arguments:
- bucket_of: int32 [16], replicated, may hold values from 0 to 3, as said below
- lengths: int32 [4], replicated, may hold values from 256 to 1024, as said below
- counts: int32 [4], replicated, may hold values from 256 to 4096
- queries: bfloat16 [32768, 4096], P(('grp', 'sp')), may hold values from -4.5 to 4.5
- keys: bfloat16 [32768, 4096], P(('grp', 'sp')), may hold values from -4.5 to 4.5
- values: bfloat16 [32768, 4096], P(('grp', 'sp')), may hold values from -6 to 6
- out_grad: bfloat16 [32768, 3072], P(('grp', 'sp')), may hold values from -24 to 24
- w_out: bfloat16 [4096, 3072], P('sp', 'grp'), may hold values from -1.75 to 1.75
Outputs:
- grad_queries: bfloat16 [32768, 4096], P(('grp', 'sp'))
- grad_keys: bfloat16 [32768, 4096], P(('grp', 'sp'))
- grad_values: bfloat16 [32768, 4096], P(('grp', 'sp'))
- grad_w_out: float32 [4096, 3072], P('sp', 'grp')
Inputs may be any that keep to these rules, and one draw needn't show every extreme that they name: `bucket_of`: every one of the 4 buckets is held by at least one group. `lengths`: one bucket has length exactly 1024.
All inputs are finite; a program needn't handle non-finite values.
Results may differ from a plain program's by a relative error of at most 0.0091.
Values may be sent and summed in bfloat16 or wider, within the bound.
A program may use at most 128 MiB of HBM per device.

v0:
```python
import jax
import jax.numpy as jnp
from jax import lax
from jax.sharding import PartitionSpec as P

HEAD_DIM = 128
SEQS = 2


def copy_for_each(shard, axis):
    devices = lax.axis_size(axis)
    return lax.all_to_all(
        jnp.broadcast_to(shard[None], (devices, *shard.shape)), axis, 0, 0, tiled=True
    )


def joined_along(pieces, dim):
    lengths = list(pieces.shape[1:])
    lengths[dim] *= pieces.shape[0]
    return jnp.moveaxis(pieces, 0, dim).reshape(lengths)


def gather_directly(shard, axis, dim):
    pieces = copy_for_each(shard, axis)
    return joined_along(pieces, dim)


def dot_nt(first_op, second_op):
    return lax.dot_general(
        first_op, second_op, (((1,), (1,)), ((), ())), preferred_element_type=jnp.float32
    )


def dot_tn(first_op, second_op):
    return lax.dot_general(
        first_op, second_op, (((0,), (0,)), ((), ())), preferred_element_type=jnp.float32
    )


def probabilities(query_rows, key_rows, keep_cols):
    scores = dot_nt(query_rows, key_rows) * query_rows.shape[1] ** (-0.5)
    scores = jnp.where(keep_cols[None, :], scores, -jnp.inf)
    row_top = jnp.max(scores, axis=1, keepdims=True)
    row_exp = jnp.exp(scores - row_top)
    return row_exp / jnp.sum(row_exp, axis=1, keepdims=True)


def shards(bucket_of, lengths, counts, queries, keys, values, out_grad, w_out):
    group_index = lax.axis_index("grp")
    number_groups = lax.axis_size("grp")
    bucket_count = lengths.shape[0]
    bucket_table = (
        bucket_of[:, None] == jnp.arange(bucket_count, dtype=jnp.int32)[None, :]
    ).astype(jnp.int32)
    group_counts = jnp.sum(bucket_table * counts[None, :], axis=1)
    group_lengths = jnp.sum(bucket_table * lengths[None, :], axis=1)
    own_group = (jnp.arange(number_groups, dtype=jnp.int32) == group_index).astype(jnp.int32)
    seq_len = jnp.sum(own_group * group_lengths)
    weight = jnp.sum(own_group * group_counts).astype(jnp.float32) / jnp.sum(group_counts).astype(
        jnp.float32
    )
    heads_q, heads_k, heads_v = (
        lax.all_to_all(queries, "sp", split_axis=1, concat_axis=0, tiled=True),
        lax.all_to_all(keys, "sp", split_axis=1, concat_axis=0, tiled=True),
        lax.all_to_all(values, "sp", split_axis=1, concat_axis=0, tiled=True),
    )
    group_rows = heads_q.shape[0]
    width_local = heads_q.shape[1]
    capacity = group_rows // SEQS
    local_heads = width_local // HEAD_DIM
    item_count = SEQS * local_heads
    keep_cols = jnp.arange(capacity, dtype=jnp.int32) < seq_len
    keep_rows = jnp.tile(keep_cols, SEQS)
    row_scale = keep_rows[:, None].astype(jnp.float32)

    def item_corner(item_index):
        return (item_index // local_heads * capacity, item_index % local_heads * HEAD_DIM)

    def take_item(source, row_first, col_first):
        return lax.dynamic_slice(source, (row_first, col_first), (capacity, HEAD_DIM))

    def forward_item(item_index, attn_all):
        row_first, col_first = item_corner(item_index)
        query_rows = take_item(heads_q, row_first, col_first)
        key_rows = take_item(heads_k, row_first, col_first)
        value_rows = take_item(heads_v, row_first, col_first)
        probs_low = probabilities(query_rows, key_rows, keep_cols).astype(jnp.bfloat16)
        attn_item = jnp.dot(probs_low, value_rows, preferred_element_type=jnp.float32).astype(
            jnp.bfloat16
        )
        return lax.dynamic_update_slice(attn_all, attn_item, (row_first, col_first))

    attention = lax.fori_loop(
        0, item_count, forward_item, jnp.zeros((group_rows, width_local), jnp.bfloat16)
    )
    masked = attention * keep_rows[:, None].astype(jnp.bfloat16)
    w_rows = gather_directly(w_out, "grp", 1)
    gathered = lax.all_gather(out_grad, "sp", axis=0, tiled=True)
    d_full = dot_nt(gathered, w_rows)
    grad_local = dot_tn(masked, gathered)
    d_attn = (d_full * row_scale).astype(jnp.bfloat16)

    def backward_item(item_index, grad_heads):
        grad_q_all, grad_k_all, grad_v_all = grad_heads
        row_first, col_first = item_corner(item_index)
        query_rows = take_item(heads_q, row_first, col_first)
        key_rows = take_item(heads_k, row_first, col_first)
        value_rows = take_item(heads_v, row_first, col_first)
        attn_item = take_item(attention, row_first, col_first)
        d_item = take_item(d_attn, row_first, col_first)
        probs_full = probabilities(query_rows, key_rows, keep_cols)
        probs_low = probs_full.astype(jnp.bfloat16)
        row_delta = jnp.sum(
            d_item.astype(jnp.float32) * attn_item.astype(jnp.float32), axis=1, keepdims=True
        )
        dscore = (probs_full * (dot_nt(d_item, value_rows) - row_delta)).astype(jnp.bfloat16)
        factor = HEAD_DIM ** (-0.5)
        grad_q = (jnp.dot(dscore, key_rows, preferred_element_type=jnp.float32) * factor).astype(
            jnp.bfloat16
        )
        grad_k = (dot_tn(dscore, query_rows) * factor).astype(jnp.bfloat16)
        grad_v = dot_tn(probs_low, d_item).astype(jnp.bfloat16)
        grad_q_all = lax.dynamic_update_slice(grad_q_all, grad_q, (row_first, col_first))
        grad_k_all = lax.dynamic_update_slice(grad_k_all, grad_k, (row_first, col_first))
        grad_v_all = lax.dynamic_update_slice(grad_v_all, grad_v, (row_first, col_first))
        return (grad_q_all, grad_k_all, grad_v_all)

    empty_heads = jnp.zeros((group_rows, width_local), jnp.bfloat16)
    grad_q_all, grad_k_all, grad_v_all = lax.fori_loop(
        0, item_count, backward_item, (empty_heads, empty_heads, empty_heads)
    )
    back_q, back_k, back_v = (
        lax.all_to_all(grad_q_all, "sp", split_axis=0, concat_axis=1, tiled=True),
        lax.all_to_all(grad_k_all, "sp", split_axis=0, concat_axis=1, tiled=True),
        lax.all_to_all(grad_v_all, "sp", split_axis=0, concat_axis=1, tiled=True),
    )
    weighted = weight * grad_local
    grad_w = lax.psum_scatter(weighted, "grp", scatter_dimension=1, tiled=True)
    return (back_q, back_k, back_v, grad_w)


def solution(mesh):
    in_specs = (
        P(),
        P(),
        P(),
        P(("grp", "sp"), None),
        P(("grp", "sp"), None),
        P(("grp", "sp"), None),
        P(("grp", "sp"), None),
        P("sp", "grp"),
    )
    out_specs = (
        P(("grp", "sp"), None),
        P(("grp", "sp"), None),
        P(("grp", "sp"), None),
        P("sp", "grp"),
    )
    return jax.shard_map(shards, mesh=mesh, in_specs=in_specs, out_specs=out_specs, check_vma=False)
```

profile of v0, /device:TPU:8, one launch (start us, length us, event | category | flops | bytes accessed | tf_op | source)
XLA Modules:
  0.0 414.1 jit_solution(11999893446016128008)
XLA Ops:
  7.9 2.4 copy.64
  10.3 11.0 %all-to-all-start = ((bf16[128,16,256]{2,0,1:T(8,128)(2,1)}), bf16[128,16,256]{2,0,1:T(8,128)(2,1)S(1)}, u32[]{:S(2)}, u32[]{:S(2)}) async-start(bf16[128,16,256]{2,0,1:T(8,128)(2,1)} %bitcast.48), calls=%async_computation | async-start | bytes 2097152 | tf_op jit(solution)/shard_map/all_to_all | solution.py:63
  22.5 35.2 %all-to-all-done = bf16[128,16,256]{2,0,1:T(8,128)(2,1)S(1)} async-done(((bf16[128,16,256]{2,0,1:T(8,128)(2,1)}), bf16[128,16,256]{2,0,1:T(8,128)(2,1)S(1)}, u32[]{:S(2)}, u32[]{:S(2)}) %all-to-all-start) | async-done | bytes 1048608 | tf_op jit(solution)/shard_map/all_to_all | solution.py:63
  57.7 12.6 %all-to-all-start.1 = ((bf16[128,16,256]{2,0,1:T(8,128)(2,1)}), bf16[128,16,256]{2,0,1:T(8,128)(2,1)S(1)}, u32[]{:S(2)}, u32[]{:S(2)}) async-start(bf16[128,16,256]{2,0,1:T(8,128)(2,1)} %bitcast.47), calls=%async_computation.1 | async-start | bytes 2097152 | tf_op jit(solution)/shard_map/all_to_all | solution.py:64
  71.4 27.0 %all-to-all-done.1 = bf16[128,16,256]{2,0,1:T(8,128)(2,1)S(1)} async-done(((bf16[128,16,256]{2,0,1:T(8,128)(2,1)}), bf16[128,16,256]{2,0,1:T(8,128)(2,1)S(1)}, u32[]{:S(2)}, u32[]{:S(2)}) %all-to-all-start.1) | async-done | bytes 1048608 | tf_op jit(solution)/shard_map/all_to_all | solution.py:64
  98.4 6.2 %all-to-all-start.3 = ((bf16[128,16,256]{2,0,1:T(8,128)(2,1)}), bf16[128,16,256]{2,0,1:T(8,128)(2,1)S(1)}, u32[]{:S(2)}, u32[]{:S(2)}) async-start(bf16[128,16,256]{2,0,1:T(8,128)(2,1)} %bitcast.46), calls=%async_computation.3 | async-start | bytes 2097152 | tf_op jit(solution)/shard_map/all_to_all | solution.py:65
  108.6 45.1 %all-to-all-done.3 = bf16[128,16,256]{2,0,1:T(8,128)(2,1)S(1)} async-done(((bf16[128,16,256]{2,0,1:T(8,128)(2,1)}), bf16[128,16,256]{2,0,1:T(8,128)(2,1)S(1)}, u32[]{:S(2)}, u32[]{:S(2)}) %all-to-all-start.3) | async-done | bytes 1048608 | tf_op jit(solution)/shard_map/all_to_all | solution.py:65
  155.2 7.9 %all-to-all-start.2 = ((bf16[16,256,192]{1,2,0:T(8,128)(2,1)}), bf16[16,256,192]{1,2,0:T(8,128)(2,1)}, u32[]{:S(2)}, u32[]{:S(2)}) async-start(bf16[16,256,192]{1,2,0:T(8,128)(2,1)} %broadcast_in_dim.87), calls=%async_computation.2 | async-start | bytes 3145728 | tf_op jit(solution)/shard_map/all_to_all | solution.py:12
  163.2 19.5 %while.36 = (s32[]{:T(128)}, bf16[2048,256]{1,0:T(8,128)(2,1)S(1)}, bf16[2048,256]{1,0:T(8,128)(2,1)S(1)}, bf16[2048,256]{1,0:T(8,128)(2,1)S(1)}, bf16[2048,256]...) while((s32[]{:T(128)}, bf16[2048,256]{1,0:T(8,128)(2,1)S(1)}, ...), condition=%wide.region_5.6_spmd.clone, body=%wide.region_2.5_spmd.clone.sunk | while | flops 549583872 | bytes 13660512 | solution.py:93
  165.5 2.5 fusion.71
  170.4 2.5 fusion.71
  175.3 2.5 fusion.71
  180.1 2.5 fusion.71
  182.7 56.8 %all-gather.2.cloned.1.call-done = bf16[2048,3072]{1,0:T(8,128)(2,1)} async-done(((bf16[128,3072]{1,0:T(8,128)(2,1)}), bf16[2048,3072]{1,0:T(8,128)(2,1)}) %all-gather.2.cloned.1.call-update) | async-done | bytes 12582928 | tf_op jit(solution)/shard_map/all_gather | solution.py:98
  239.5 11.6 %convolution_multiply_fusion.2 = f32[256,3072]{0,1:T(8,128)} fusion(bf16[2048,3072]{1,0:T(8,128)(2,1)} %all-gather.2.cloned.1.call-done, f32[]{:T(128)S(6)} %div.66, bf16[2048,256]{1,0:T(8,128)(2,1)S(1)} %get-tuple-element.655, bf16[2048]{0:T(1024)(128)(2,1)S(1)} %bitcast.67), kind=kOutput, calls=%fused_computation.43 | convolution fusion | flops 3222536192 | bytes 16781316 | tf_op jit(solution)/shard_map/dot_general | solution.py:35
  251.1 9.5 %fusion.39 = bf16[2048,256]{1,0:T(8,128)(2,1)} fusion(bf16[2048,3072]{1,0:T(8,128)(2,1)} %all-gather.2.cloned.1.call-done, bf16[256,3072]{0,1:T(8,128)(2,1)} %bitcast.5, f32[2048]{0:T(1024)S(1)} %bitcast.66), kind=kOutput, calls=%fused_computation.45 | convolution fusion | flops 3222274048 | bytes 15212544 | tf_op jit(solution)/shard_map/dot_general | solution.py:29
  263.7 42.5 %while.37 = (s32[]{:T(128)}, bf16[2048,256]{1,0:T(8,128)(2,1)}, bf16[2048,256]{1,0:T(8,128)(2,1)}, bf16[2048,256]{1,0:T(8,128)(2,1)}, bf16[2048,256]{1,0:T(8,128...) while((s32[]{:T(128)}, bf16[2048,256]{1,0:T(8,128)(2,1)}, ...), condition=%wide.region_10.11_spmd.clone, body=%wide.region_6.10_spmd.clone.sunk | while | flops 1363277824 | bytes 30461348 | solution.py:129
  267.1 1.9 fusion.84
  269.0 2.4 multiply_convert_fusion.2
  277.8 1.9 fusion.84
  279.7 2.4 multiply_convert_fusion.2
  283.4 1.5 fusion.82
  288.4 1.9 fusion.84
  290.3 2.4 multiply_convert_fusion.2
  299.0 1.9 fusion.84
  300.9 2.4 multiply_convert_fusion.2
  304.7 1.5 fusion.82
  306.2 33.9 %all_to_all.119 = bf16[16,128,256]{2,1,0:T(8,128)(2,1)S(1)} all-to-all(bf16[16,128,256]{2,1,0:T(8,128)(2,1)} %bitcast.58), channel_id=1, replica_groups=mesh['grp'=16,'sp'=16] {'sp'}, dimensions={0} | all-to-all | bytes 2097152 | tf_op jit(solution)/shard_map/all_to_all | solution.py:133
  340.1 34.0 %all_to_all.120 = bf16[16,128,256]{2,1,0:T(8,128)(2,1)S(1)} all-to-all(bf16[16,128,256]{2,1,0:T(8,128)(2,1)} %bitcast.57), channel_id=1, replica_groups=mesh['grp'=16,'sp'=16] {'sp'}, dimensions={0} | all-to-all | bytes 2097152 | tf_op jit(solution)/shard_map/all_to_all | solution.py:135
  374.1 4.4 %all-to-all-start.5 = ((bf16[16,128,256]{2,1,0:T(8,128)(2,1)}), bf16[16,128,256]{2,1,0:T(8,128)(2,1)S(1)}, u32[]{:S(2)}, u32[]{:S(2)}) async-start(bf16[16,128,256]{2,1,0:T(8,128)(2,1)} %bitcast.14), calls=%async_computation.5 | async-start | bytes 2097152 | tf_op jit(solution)/shard_map/all_to_all | solution.py:134
  379.8 2.3 copy.48
  384.0 21.3 %all-to-all-done.5 = bf16[16,128,256]{2,1,0:T(8,128)(2,1)S(1)} async-done(((bf16[16,128,256]{2,1,0:T(8,128)(2,1)}), bf16[16,128,256]{2,1,0:T(8,128)(2,1)S(1)}, u32[]{:S(2)}, u32[]{:S(2)}) %all-to-all-start.5) | async-done | bytes 1048608 | tf_op jit(solution)/shard_map/all_to_all | solution.py:134
  (82 shorter events, 46.9 us)
Async XLA Ops:
  7.2 14.2 %copy-start.1 = (bf16[128,4096]{1,0:T(8,128)(2,1)S(1)}, bf16[128,4096]{1,0:T(8,128)(2,1)}, u32[]{:S(2)}) copy-start(bf16[128,4096]{1,0:T(8,128)(2,1)} %param.16) | copy-start | bytes 3145732
  7.2 232.3 %all-gather.2.cloned.1.call-start = ((), (), s32[]{:S(2)}) async-start(), calls=%async_computation.8 | async-start | bytes 13369344 | tf_op jit(solution)/shard_map/all_gather | solution.py:98
  7.9 62.4 %copy-start.2 = (bf16[128,4096]{1,0:T(8,128)(2,1)S(1)}, bf16[128,4096]{1,0:T(8,128)(2,1)}, u32[]{:S(2)}) copy-start(bf16[128,4096]{1,0:T(8,128)(2,1)} %param.17) | copy-start | bytes 3145732
  10.3 47.4 %all-to-all-start = ((bf16[128,16,256]{2,0,1:T(8,128)(2,1)}), bf16[128,16,256]{2,0,1:T(8,128)(2,1)S(1)}, u32[]{:S(2)}, u32[]{:S(2)}) async-start(bf16[128,16,256]{2,0,1:T(8,128)(2,1)} %bitcast.48), calls=%async_computation | async-start | bytes 2097152 | tf_op jit(solution)/shard_map/all_to_all | solution.py:63
  21.4 83.3 %copy-start.5 = (s32[4]{0:T(128)S(1)}, s32[4]{0:T(128)}, u32[]{:S(2)}) copy-start(s32[4]{0:T(128)} %param.14) | copy-start | bytes 52
  21.4 83.2 %copy-start.6 = (s32[16]{0:T(128)S(1)}, s32[16]{0:T(128)}, u32[]{:S(2)}) copy-start(s32[16]{0:T(128)} %param.12) | copy-start | bytes 196
  21.4 83.2 %copy-start.7 = (s32[4]{0:T(128)S(1)}, s32[4]{0:T(128)}, u32[]{:S(2)}) copy-start(s32[4]{0:T(128)} %param.13) | copy-start | bytes 52
  21.4 132.4 %copy-start.4 = (bf16[256,192]{0,1:T(8,128)(2,1)S(1)}, bf16[256,192]{0,1:T(8,128)(2,1)}, u32[]{:S(2)}) copy-start(bf16[256,192]{0,1:T(8,128)(2,1)} %param.19) | copy-start | bytes 294916
  57.7 40.7 %all-to-all-start.1 = ((bf16[128,16,256]{2,0,1:T(8,128)(2,1)}), bf16[128,16,256]{2,0,1:T(8,128)(2,1)S(1)}, u32[]{:S(2)}, u32[]{:S(2)}) async-start(bf16[128,16,256]{2,0,1:T(8,128)(2,1)} %bitcast.47), calls=%async_computation.1 | async-start | bytes 2097152 | tf_op jit(solution)/shard_map/all_to_all | solution.py:64
  98.4 55.3 %all-to-all-start.3 = ((bf16[128,16,256]{2,0,1:T(8,128)(2,1)}), bf16[128,16,256]{2,0,1:T(8,128)(2,1)S(1)}, u32[]{:S(2)}, u32[]{:S(2)}) async-start(bf16[128,16,256]{2,0,1:T(8,128)(2,1)} %bitcast.46), calls=%async_computation.3 | async-start | bytes 2097152 | tf_op jit(solution)/shard_map/all_to_all | solution.py:65
  153.8 9.4 %copy-start.3 = (bf16[128,16,256]{2,0,1:T(8,128)(2,1)}, bf16[128,16,256]{2,0,1:T(8,128)(2,1)S(1)}, u32[]{:S(2)}) copy-start(bf16[128,16,256]{2,0,1:T(8,128)(2,1)S(1)} %all-to-all-done.3) | copy-start | bytes 3145732
  155.2 95.8 %all-to-all-start.2 = ((bf16[16,256,192]{1,2,0:T(8,128)(2,1)}), bf16[16,256,192]{1,2,0:T(8,128)(2,1)}, u32[]{:S(2)}, u32[]{:S(2)}) async-start(bf16[16,256,192]{1,2,0:T(8,128)(2,1)} %broadcast_in_dim.87), calls=%async_computation.2 | async-start | bytes 3145728 | tf_op jit(solution)/shard_map/all_to_all | solution.py:12
  163.1 244.1 %reduce-scatter.2.cloned.1.call-start = ((), (), s32[]{:S(2)}) async-start(), calls=%async_computation.9 | async-start | bytes 3342336 | tf_op jit(solution)/shard_map/reduce_scatter | solution.py:138
  265.5 1.7 copy-start
  276.1 1.7 copy-start
  286.7 1.7 copy-start
  297.4 1.7 copy-start
  374.1 31.2 %all-to-all-start.5 = ((bf16[16,128,256]{2,1,0:T(8,128)(2,1)}), bf16[16,128,256]{2,1,0:T(8,128)(2,1)S(1)}, u32[]{:S(2)}, u32[]{:S(2)}) async-start(bf16[16,128,256]{2,1,0:T(8,128)(2,1)} %bitcast.14), calls=%async_computation.5 | async-start | bytes 2097152 | tf_op jit(solution)/shard_map/all_to_all | solution.py:134
Sparse Core Ops, SparseCore 0:
  10.4 229.0 all-gather.1
  251.2 61.2 reduce-scatter.1
where the time goes:
time: 415 us; the launch traced here: 414 us
  waiting for transfers between devices  186 us (45%)
  blocking collectives  67.9 us (16%)
  matrix products  65.6 us (16%)
  starting transfers between devices  42.1 us (10%)
  other arithmetic  19.5 us (5%)
  local copies, waits for them, and re-layouts  16.8 us (4%)
  between operations  15.6 us (4%)
    all_gather x1, waiting for transfers between devices, shards(): gathered = lax.all_gather(out_grad, 'sp', axis=0, tiled=True)  56.8 us
    all_to_all x1, waiting for transfers between devices, shards(): lax.all_to_all(values, 'sp', split_axis=1, concat_axis=0, tiled=True)  45.1 us
    all_to_all x1, waiting for transfers between devices, shards(): lax.all_to_all(queries, 'sp', split_axis=1, concat_axis=0, tiled=True)  35.2 us
    all_to_all x1, blocking collectives, shards(): lax.all_to_all(grad_v_all, 'sp', split_axis=0, concat_axis=1, tiled=True)  34 us
    all_to_all x1, blocking collectives, shards(): lax.all_to_all(grad_q_all, 'sp', split_axis=0, concat_axis=1, tiled=True)  33.9 us
    all_to_all x1, waiting for transfers between devices, shards(): lax.all_to_all(keys, 'sp', split_axis=1, concat_axis=0, tiled=True)  27 us
    dot_general x9, matrix products, dot_tn(): lax.dot_general(first_op, second_op, (((0,), (0,)), ((), ())), preferred_...  24.8 us
    dot_general x13, matrix products, dot_nt(): lax.dot_general(first_op, second_op, (((1,), (1,)), ((), ())), preferred_...  24.8 us
  transfers between devices with their start and end apart: 7, of which 5 were waited for; matrix products, arithmetic and copies ran while one was open for 25% of the time, Pallas kernels for 0%

commit v1 on v0

--- a/solution.py
+++ b/solution.py
@@ -95,7 +95,9 @@
     )
     masked = attention * keep_rows[:, None].astype(jnp.bfloat16)
     w_rows = gather_directly(w_out, "grp", 1)
-    gathered = lax.all_gather(out_grad, "sp", axis=0, tiled=True)
+    gathered = jnp.concatenate(
+        lax.all_to_all(jnp.stack([out_grad] * lax.axis_size("sp")), "sp", 0, 0), axis=0
+    )
     d_full = dot_nt(gathered, w_rows)
     grad_local = dot_tn(masked, gathered)
     d_attn = (d_full * row_scale).astype(jnp.bfloat16)

time: 415 us -> 619 us (1.49)
  waiting for transfers between devices: 186 us -> 354 us
  blocking collectives: 67.9 us -> 97.3 us
  local copies, waits for them, and re-layouts: 16.8 us -> 24.1 us
    all_to_all x2, waiting for transfers between devices: 66.4 us -> 301 us  [the longest x1 282 us: shards(): lax.all_to_all(jnp.stack([out_grad] * lax.axis_size('sp')), 'sp', 0, 0)]
    all_gather x1 -> x0, waiting for transfers between devices: 56.8 us -> none  [shards(): gathered = lax.all_gather(out_grad, 'sp', axis=0, tiled=True)]
    all_to_all x1 -> x2, blocking collectives: 34 us -> 62.8 us  [the longest x1 34 us: shards(): lax.all_to_all(values, 'sp', split_axis=1, concat_axis=0, tiled=True)]
    all_to_all x1, waiting for transfers between devices: 35.2 us -> 26.8 us  [shards(): lax.all_to_all(queries, 'sp', split_axis=1, concat_axis=0, tiled=True)]
    another operation x4 -> x5, local copies, waits for them, and re-layouts: 3.19 us -> 10.4 us  [the longest x1 7.2 us: shards(): jnp.stack([out_grad] * lax.axis_size('sp'))]
    all_to_all x1, starting transfers between devices: 12.6 us -> 5.95 us  [shards(): lax.all_to_all(keys, 'sp', split_axis=1, concat_axis=0, tiled=True)]
  transfers between devices with their start and end apart: 7 -> 6, of which waited for: 5 -> 4; matrix products, arithmetic and copies ran while one was open for 25% -> 16% of each run, Pallas kernels for 0% -> 0%
where the time goes in v1:
time: 619 us; the launch traced here: 612 us
  waiting for transfers between devices  354 us (57%)
  blocking collectives  97.3 us (16%)
  matrix products  65.8 us (11%)
  starting transfers between devices  38.3 us (6%)
  local copies, waits for them, and re-layouts  24.1 us (4%)
  other arithmetic  16.4 us (3%)
  between operations  15.5 us (3%)
    all_to_all x1, waiting for transfers between devices, shards(): lax.all_to_all(jnp.stack([out_grad] * lax.axis_size('sp')), 'sp', 0, 0)  282 us
    all_to_all x1, blocking collectives, shards(): lax.all_to_all(grad_q_all, 'sp', split_axis=0, concat_axis=1, tiled=True)  34.5 us
    all_to_all x1, blocking collectives, shards(): lax.all_to_all(values, 'sp', split_axis=1, concat_axis=0, tiled=True)  34 us
    all_to_all x1, blocking collectives, shards(): lax.all_to_all(grad_k_all, 'sp', split_axis=0, concat_axis=1, tiled=True)  28.8 us
    all_to_all x1, waiting for transfers between devices, shards(): lax.all_to_all(queries, 'sp', split_axis=1, concat_axis=0, tiled=True)  26.8 us
    all_to_all x1, waiting for transfers between devices, shards(): lax.all_to_all(keys, 'sp', split_axis=1, concat_axis=0, tiled=True)  26.2 us
    dot_general x9, matrix products, dot_tn(): lax.dot_general(first_op, second_op, (((0,), (0,)), ((), ())), preferred_...  24.9 us
    dot_general x13, matrix products, dot_nt(): lax.dot_general(first_op, second_op, (((1,), (1,)), ((), ())), preferred_...  24.8 us
  transfers between devices with their start and end apart: 6, of which 4 were waited for; matrix products, arithmetic and copies ran while one was open for 16% of the time, Pallas kernels for 0%

profile of v1, /device:TPU:8, one launch (start us, length us, event | category | flops | bytes accessed | tf_op | source)
XLA Modules:
  0.0 612.0 jit_solution(17398223046747891048)
XLA Ops:
  7.2 2.4 copy.64
  9.6 11.0 %all-to-all-start = ((bf16[128,16,256]{2,0,1:T(8,128)(2,1)}), bf16[128,16,256]{2,0,1:T(8,128)(2,1)S(1)}, u32[]{:S(2)}, u32[]{:S(2)}) async-start(bf16[128,16,256]{2,0,1:T(8,128)(2,1)} %bitcast.49), calls=%async_computation | async-start | bytes 2097152 | tf_op jit(solution)/shard_map/all_to_all | solution.py:63
  21.7 26.8 %all-to-all-done = bf16[128,16,256]{2,0,1:T(8,128)(2,1)S(1)} async-done(((bf16[128,16,256]{2,0,1:T(8,128)(2,1)}), bf16[128,16,256]{2,0,1:T(8,128)(2,1)S(1)}, u32[]{:S(2)}, u32[]{:S(2)}) %all-to-all-start) | async-done | bytes 1048608 | tf_op jit(solution)/shard_map/all_to_all | solution.py:63
  48.5 5.9 all-to-all-start.1
  55.8 26.2 %all-to-all-done.1 = bf16[128,16,256]{2,0,1:T(8,128)(2,1)S(1)} async-done(((bf16[128,16,256]{2,0,1:T(8,128)(2,1)}), bf16[128,16,256]{2,0,1:T(8,128)(2,1)S(1)}, u32[]{:S(2)}, u32[]{:S(2)}) %all-to-all-start.1) | async-done | bytes 1048608 | tf_op jit(solution)/shard_map/all_to_all | solution.py:64
  82.0 34.0 %all_to_all.124 = bf16[128,16,256]{2,0,1:T(8,128)(2,1)} all-to-all(bf16[128,16,256]{2,0,1:T(8,128)(2,1)S(1)} %bitcast.58), channel_id=1, replica_groups=mesh['grp'=16,'sp'=16] {'sp'}, dimensions={1} | all-to-all | bytes 2097152 | tf_op jit(solution)/shard_map/all_to_all | solution.py:65
  116.0 7.2 %stack.2 = bf16[16,128,3072]{2,1,0:T(8,128)(2,1)} broadcast(bf16[128,3072]{1,0:T(8,128)(2,1)} %param.18), dimensions={1,2} | broadcast | bytes 13369344 | tf_op jit(solution)/shard_map/stack | solution.py:99
  123.2 5.1 all-to-all-start.2
  132.5 282.2 %all-to-all-done.2 = bf16[16,128,3072]{2,1,0:T(8,128)(2,1)} async-done(((bf16[16,128,3072]{2,1,0:T(8,128)(2,1)}), bf16[16,128,3072]{2,1,0:T(8,128)(2,1)}, u32[]{:S(2)}, u32[]{:S(2)}) %all-to-all-start.2) | async-done | bytes 12582944 | tf_op jit(solution)/shard_map/all_to_all | solution.py:99
  416.0 4.9 all-to-all-start.3
  421.3 19.7 %while.36 = (s32[]{:T(128)}, bf16[2048,256]{1,0:T(8,128)(2,1)S(1)}, bf16[2048,256]{1,0:T(8,128)(2,1)S(1)}, bf16[2048,256]{1,0:T(8,128)(2,1)S(1)}, bf16[2048,256]...) while((s32[]{:T(128)}, bf16[2048,256]{1,0:T(8,128)(2,1)S(1)}, ...), condition=%wide.region_5.6_spmd.clone, body=%wide.region_2.5_spmd.clone.sunk | while | flops 549583872 | bytes 13660504 | solution.py:93
  423.6 2.5 fusion.71
  428.6 2.5 fusion.71
  433.5 2.5 fusion.71
  438.5 2.5 fusion.71
  441.0 11.6 %convolution_multiply_fusion.2 = f32[256,3072]{0,1:T(8,128)} fusion(bf16[2048,3072]{1,0:T(8,128)(2,1)} %bitcast.4, f32[]{:T(128)S(6)} %div.66, bf16[2048,256]{1,0:T(8,128)(2,1)S(1)} %get-tuple-element.655, bf16[2048]{0:T(1024)(128)(2,1)S(1)} %bitcast.67), kind=kOutput, calls=%fused_computation.43 | convolution fusion | flops 3222536192 | bytes 16781316 | tf_op jit(solution)/shard_map/dot_general | solution.py:35
  452.6 9.5 %fusion.39 = bf16[2048,256]{1,0:T(8,128)(2,1)} fusion(bf16[2048,3072]{1,0:T(8,128)(2,1)} %bitcast.4, bf16[256,3072]{0,1:T(8,128)(2,1)} %bitcast.6, f32[2048]{0:T(1024)S(1)} %bitcast.66), kind=kOutput, calls=%fused_computation.45 | convolution fusion | flops 3222274048 | bytes 15212544 | tf_op jit(solution)/shard_map/dot_general | solution.py:29
  465.2 39.1 %while.37 = (s32[]{:T(128)}, bf16[2048,256]{1,0:T(8,128)(2,1)}, bf16[2048,256]{1,0:T(8,128)(2,1)}, bf16[2048,256]{1,0:T(8,128)(2,1)}, bf16[2048,256]{1,0:T(8,128...) while((s32[]{:T(128)}, bf16[2048,256]{1,0:T(8,128)(2,1)}, ...), condition=%wide.region_10.11_spmd.clone, body=%wide.region_6.10_spmd.clone.sunk | while | flops 1363277824 | bytes 30461340 | solution.py:131
  467.6 1.9 fusion.84
  469.7 2.4 multiply_convert_fusion.2
  477.4 1.9 fusion.84
  479.5 2.4 multiply_convert_fusion.2
  483.3 1.5 fusion.82
  487.1 1.9 fusion.84
  489.3 2.4 multiply_convert_fusion.2
  496.9 1.9 fusion.84
  499.0 2.4 multiply_convert_fusion.2
  504.3 34.5 %all_to_all.125 = bf16[16,128,256]{2,1,0:T(8,128)(2,1)S(1)} all-to-all(bf16[16,128,256]{2,1,0:T(8,128)(2,1)} %bitcast.12), channel_id=1, replica_groups=mesh['grp'=16,'sp'=16] {'sp'}, dimensions={0} | all-to-all | bytes 2097152 | tf_op jit(solution)/shard_map/all_to_all | solution.py:135
  538.8 28.8 %all_to_all.126 = bf16[16,128,256]{2,1,0:T(8,128)(2,1)S(1)} all-to-all(bf16[16,128,256]{2,1,0:T(8,128)(2,1)} %bitcast.15), channel_id=1, replica_groups=mesh['grp'=16,'sp'=16] {'sp'}, dimensions={0} | all-to-all | bytes 2097152 | tf_op jit(solution)/shard_map/all_to_all | solution.py:136
  567.7 11.1 %all-to-all-start.7 = ((bf16[16,128,256]{2,1,0:T(8,128)(2,1)}), bf16[16,128,256]{2,1,0:T(8,128)(2,1)S(1)}, u32[]{:S(2)}, u32[]{:S(2)}) async-start(bf16[16,128,256]{2,1,0:T(8,128)(2,1)} %bitcast.18), calls=%async_computation.7 | async-start | bytes 2097152 | tf_op jit(solution)/shard_map/all_to_all | solution.py:137
  580.1 2.3 copy.48
  584.3 18.9 %all-to-all-done.7 = bf16[16,128,256]{2,1,0:T(8,128)(2,1)S(1)} async-done(((bf16[16,128,256]{2,1,0:T(8,128)(2,1)}), bf16[16,128,256]{2,1,0:T(8,128)(2,1)S(1)}, u32[]{:S(2)}, u32[]{:S(2)}) %all-to-all-start.7) | async-done | bytes 1048608 | tf_op jit(solution)/shard_map/all_to_all | solution.py:137
  (77 shorter events, 44.9 us)
Async XLA Ops:
  7.2 13.4 %copy-start.1 = (bf16[128,4096]{1,0:T(8,128)(2,1)S(1)}, bf16[128,4096]{1,0:T(8,128)(2,1)}, u32[]{:S(2)}) copy-start(bf16[128,4096]{1,0:T(8,128)(2,1)} %param.16) | copy-start | bytes 3145732
  9.6 38.9 %all-to-all-start = ((bf16[128,16,256]{2,0,1:T(8,128)(2,1)}), bf16[128,16,256]{2,0,1:T(8,128)(2,1)S(1)}, u32[]{:S(2)}, u32[]{:S(2)}) async-start(bf16[128,16,256]{2,0,1:T(8,128)(2,1)} %bitcast.49), calls=%async_computation | async-start | bytes 2097152 | tf_op jit(solution)/shard_map/all_to_all | solution.py:63
  48.5 33.5 %all-to-all-start.1 = ((bf16[128,16,256]{2,0,1:T(8,128)(2,1)}), bf16[128,16,256]{2,0,1:T(8,128)(2,1)S(1)}, u32[]{:S(2)}, u32[]{:S(2)}) async-start(bf16[128,16,256]{2,0,1:T(8,128)(2,1)} %bitcast.48), calls=%async_computation.1 | async-start | bytes 2097152 | tf_op jit(solution)/shard_map/all_to_all | solution.py:64
  123.2 5.1 copy-start.3
  123.2 5.1 copy-start.4
  123.2 5.1 copy-start.5
  123.2 291.5 %copy-start.2 = (bf16[256,192]{0,1:T(8,128)(2,1)S(1)}, bf16[256,192]{0,1:T(8,128)(2,1)}, u32[]{:S(2)}) copy-start(bf16[256,192]{0,1:T(8,128)(2,1)} %param.19) | copy-start | bytes 294916
  123.2 291.5 %all-to-all-start.2 = ((bf16[16,128,3072]{2,1,0:T(8,128)(2,1)}), bf16[16,128,3072]{2,1,0:T(8,128)(2,1)}, u32[]{:S(2)}, u32[]{:S(2)}) async-start(bf16[16,128,3072]{2,1,0:T(8,128)(2,1)} %stack.2), calls=%async_computation.2 | async-start | bytes 25165824 | tf_op jit(solution)/shard_map/all_to_all | solution.py:99
  416.0 36.6 %all-to-all-start.3 = ((bf16[16,256,192]{1,2,0:T(8,128)(2,1)}), bf16[16,256,192]{1,2,0:T(8,128)(2,1)}, u32[]{:S(2)}, u32[]{:S(2)}) async-start(bf16[16,256,192]{1,2,0:T(8,128)(2,1)} %broadcast_in_dim.87), calls=%async_computation.3 | async-start | bytes 3145728 | tf_op jit(solution)/shard_map/all_to_all | solution.py:12
  421.0 184.2 %reduce-scatter.2.cloned.1.call-start = ((), (), s32[]{:S(2)}) async-start(), calls=%async_computation.9 | async-start | bytes 3342336 | tf_op jit(solution)/shard_map/reduce_scatter | solution.py:140
  465.9 1.7 copy-start
  475.7 1.7 copy-start
  485.5 1.7 copy-start
  495.2 1.7 copy-start
  567.7 35.5 %all-to-all-start.7 = ((bf16[16,128,256]{2,1,0:T(8,128)(2,1)}), bf16[16,128,256]{2,1,0:T(8,128)(2,1)S(1)}, u32[]{:S(2)}, u32[]{:S(2)}) async-start(bf16[16,128,256]{2,1,0:T(8,128)(2,1)} %bitcast.18), calls=%async_computation.7 | async-start | bytes 2097152 | tf_op jit(solution)/shard_map/all_to_all | solution.py:137
Sparse Core Ops, SparseCore 0:
  452.7 64.4 reduce-scatter.1
